TPU v7x, 64 devices: a 2x2x8 block of a 4x4x8 slice. The times are simulated.
64 devices in a mesh: pod: 4 (over x, y), mp: 16 (over z, core).
Axes of the slice: x: 2, y: 2, z: 8, core: 2. Of those that a mesh axis runs over, the one named last changes fastest.
The devices are a block of a 4x4x8 slice.
Arguments:
- d_pool: bfloat16 [131072, 26, 128], P(('pod', 'mp')), parts along dimension 0
- row_ids: int32 [128, 32768, 1], P(('pod', 'mp')), parts along dimension 0
- lengths: int32 [128, 32768], P(('pod', 'mp')), parts along dimension 0
- tables: bfloat16 [128, 8192, 128], P(('pod', 'mp')), parts along dimension 0
- row_accum: float32 [128, 8192], P(('pod', 'mp')), parts along dimension 0
- learn_rate: float32 [], replicated
Outputs:
- output 1: bfloat16 [128, 8192, 128], P(('pod', 'mp')), parts along dimension 0
- output 2: float32 [128, 8192], P(('pod', 'mp')), parts along dimension 0
There are 4 independent parts. A program takes and returns all parts, laid end to end along the dimension named above; an argument that names none is the same for every part.
All inputs are finite; a program needn't handle non-finite values.
Results may differ from a plain program's by a relative error of at most 0.001.
Values are sent between devices in bfloat16 or wider.
A program may use at most 768 MiB of HBM per device.

v0:
```python
import jax
import jax.numpy as jnp
from jax import lax
from jax.sharding import PartitionSpec as P

EPSILON = 1e-06


def scatter_rows(owned_grad, row_ids, lengths, n_rows):
    slots_dev, batch_all, emb_dim = owned_grad.shape
    grad_vals = owned_grad.astype(jnp.float32).reshape(slots_dev * batch_all, emb_dim)
    row_offset = (jnp.arange(slots_dev, dtype=jnp.int32) * n_rows)[:, None]
    dropped = slots_dev * n_rows

    def add_position(pos_idx, row_grad):
        pos_ids = lax.dynamic_index_in_dim(row_ids, pos_idx, axis=2, keepdims=False)
        seg_rows = jnp.where(pos_idx < lengths, pos_ids + row_offset, dropped).reshape(-1)
        return row_grad.at[seg_rows].add(grad_vals, mode='drop')

    row_grad = lax.fori_loop(0, row_ids.shape[2], add_position, jnp.zeros((dropped, emb_dim), jnp.float32))
    return row_grad.reshape(slots_dev, n_rows, emb_dim)


def adagrad_rows(tables, row_accum, row_grad, learn_rate):
    new_accum = row_accum + jnp.mean(row_grad * row_grad, axis=-1)
    row_scale = learn_rate / (jnp.sqrt(new_accum) + EPSILON)
    new_tables = (tables.astype(jnp.float32) - row_grad * row_scale[..., None]).astype(jnp.bfloat16)
    return new_tables, new_accum


def solution(mesh):
    n_group = mesh.shape['mp']
    slot_spec = P(('pod', 'mp'))

    def local_step(d_pool, row_ids, lengths, tables, row_accum, learn_rate):
        n_tab = d_pool.shape[1]
        slots_dev = tables.shape[0]
        padded = jnp.pad(d_pool, ((0, 0), (0, slots_dev * n_group - n_tab), (0, 0)))
        owned_all = lax.all_to_all(padded, 'mp', 1, 0, tiled=True)
        owned_grad = jnp.swapaxes(owned_all, 0, 1)
        row_grad = scatter_rows(owned_grad, row_ids, lengths, tables.shape[1])
        return adagrad_rows(tables, row_accum, row_grad, learn_rate)

    return jax.shard_map(local_step, mesh=mesh, in_specs=(slot_spec, slot_spec, slot_spec, slot_spec, slot_spec, P()), out_specs=(slot_spec, slot_spec), check_vma=False)
```

profile of v0, /device:TPU:21, one launch (start us, length us, event | category | flops | bytes accessed | tf_op | source)
XLA Modules:
  0.0 789.5 jit_solution(226182722654151561)
XLA Ops:
  0.6 13.8 %pad.4 = bf16[2048,32,128]{2,0,1:T(8,128)(2,1)} pad(bf16[2048,26,128]{2,0,1:T(8,128)(2,1)} %param.6, bf16[]{:T(256)} %constant.18.clone.1), padding=0_0x0_6x0_0 | pad | bytes 30408706 | tf_op jit(solution)/shard_map/jit(_pad)/pad | solution.py:38
  14.4 0.0 copy-start
  14.4 0.0 copy-start.1
  14.4 10.9 %all-to-all-start = ((bf16[2048,32,128]{2,0,1:T(8,128)(2,1)}), bf16[2048,32,128]{2,0,1:T(8,128)(2,1)}, u32[]{:S(2)}, u32[]{:S(2)}) async-start(bf16[2048,32,128]{2,0,1:T(8,128)(2,1)} %pad.4), calls=%async_computation | async-start | bytes 33554432 | tf_op jit(solution)/shard_map/all_to_all | solution.py:39
  25.3 0.0 copy-done
  25.3 0.0 copy-done.1
  25.3 0.3 fusion.2
  25.7 0.3 copy.10
  26.6 0.3 compare_select_fusion
  26.9 378.2 %all-to-all-done = bf16[2048,32,128]{2,0,1:T(8,128)(2,1)} async-done(((bf16[2048,32,128]{2,0,1:T(8,128)(2,1)}), bf16[2048,32,128]{2,0,1:T(8,128)(2,1)}, u32[]{:S(2)}, u32[]{:S(2)}) %all-to-all-start) | async-done | bytes 16777248 | tf_op jit(solution)/shard_map/all_to_all | solution.py:39
  405.0 8.5 %convert_bitcast_fusion = f32[16,2048,2,128]{3,1,2,0:T(8,128)S(1)} fusion(bf16[2048,16,2,128]{3,0,2,1:T(8,128)(2,1)} %bitcast.7), kind=kLoop, calls=%fused_computation.1 | loop fusion | flops 8388608 | bytes 50331648 | tf_op jit(solution)/shard_map/reshape | solution.py:11
  413.6 11.0 %copy.8 = f32[16,2048,2,128]{3,1,0,2:T(8,128)} copy(f32[16,2048,2,128]{3,1,2,0:T(8,128)S(1)} %convert_bitcast_fusion) | data formatting | bytes 67108864 | tf_op jit(solution)/shard_map/reshape | solution.py:11
  424.6 0.0 copy-start.2
  424.6 351.2 %scatter_custom_fusion = f32[16384,128]{1,0:T(8,128)} fusion(s32[65536]{0:T(1024)S(1)} %bitcast.23, f32[65536,128]{1,0:T(8,128)} %bitcast.21, f32[]{:T(128)} %constant.8.clone.1), kind=kCustom, calls=%fused_computation.4 | custom fusion | flops 8388608 | bytes 8389120 | tf_op jit(solution)/shard_map/while/body/eval_jaxpr/scatter-add | solution.py:18
  775.8 4.6 multiply_reduce_fusion
  780.5 0.0 copy-done.2
  780.5 0.7 add_divide_fusion
  781.2 8.3 %subtract_convert_fusion = bf16[2,8192,128]{2,1,0:T(8,128)(2,1)} fusion(f32[2,8192,128]{2,1,0:T(8,128)} %bitcast.20, bf16[2,8192,128]{2,1,0:T(8,128)(2,1)} %param.9, f32[2,8192]{1,0:T(2,128)S(1)} %get-tuple-element.16), kind=kLoop, calls=%fused_computation.2 | loop fusion | flops 8388608 | bytes 16842752 | tf_op jit(solution)/shard_map/convert_element_type | solution.py:27
  (3 shorter events, 0.0 us)
Async XLA Ops:
  14.4 10.9 %copy-start = (s32[2,32768]{1,0:T(2,128)S(1)}, s32[2,32768]{1,0:T(2,128)}, u32[]{:S(2)}) copy-start(s32[2,32768]{1,0:T(2,128)} %param.8) | copy-start | bytes 786436
  14.4 10.9 %copy-start.1 = (s32[2,32768,1]{1,2,0:T(1,128)S(1)}, s32[2,32768,1]{1,2,0:T(1,128)}, u32[]{:S(2)}) copy-start(s32[2,32768,1]{1,2,0:T(1,128)} %param.7) | copy-start | bytes 786436
  14.4 390.6 %all-to-all-start = ((bf16[2048,32,128]{2,0,1:T(8,128)(2,1)}), bf16[2048,32,128]{2,0,1:T(8,128)(2,1)}, u32[]{:S(2)}, u32[]{:S(2)}) async-start(bf16[2048,32,128]{2,0,1:T(8,128)(2,1)} %pad.4), calls=%async_computation | async-start | bytes 33554432 | tf_op jit(solution)/shard_map/all_to_all | solution.py:39
  424.6 355.9 %copy-start.2 = (f32[2,8192]{1,0:T(2,128)S(1)}, f32[2,8192]{1,0:T(2,128)}, u32[]{:S(2)}) copy-start(f32[2,8192]{1,0:T(2,128)} %param.10) | copy-start | bytes 196612
where the time goes:
time: 790 us
  waiting for transfers between devices  378 us (48%)
  other arithmetic  374 us (47%)
  local copies, waits for them, and re-layouts  25.1 us (3%)
  starting transfers between devices  10.9 us (1%)
    all_to_all x1, waiting for transfers between devices, local_step(): owned_all = lax.all_to_all(padded, 'mp', 1, 0, tiled=True)  378 us
    scatter-add x1, other arithmetic, add_position(): return row_grad.at[seg_rows].add(grad_vals, mode='drop')  351 us
  transfers between devices with their start and end apart: 1, of which 1 were waited for; matrix products, arithmetic and copies ran while one was open for 0% of the time, Pallas kernels for 0%

commit v1 on v0

v1 whole, which is shorter than its diff:
```python
import functools

import jax
import jax.numpy as jnp
from jax import lax
from jax.experimental import pallas as pl
from jax.experimental.pallas import tpu as pltpu
from jax.sharding import PartitionSpec as P

EPSILON = 1e-06
SUB = 256
COPIES = 8
ROWS = 16


def compact_kernel(cap, start_ref, len_ref, grad_ref, out_ref, rows_ref):
    table = pl.program_id(0)
    n_sub = len_ref.shape[1]
    valid = len_ref[0]
    before = lax.broadcasted_iota(jnp.int32, (SUB, SUB), 0) < lax.broadcasted_iota(jnp.int32, (SUB, SUB), 1)
    rank = jnp.dot(valid.astype(jnp.bfloat16), before.astype(jnp.bfloat16), preferred_element_type=jnp.float32)
    rank = jnp.where(valid > 0, rank, -1.0)
    place = lax.broadcasted_iota(jnp.int32, (SUB, SUB), 0).astype(jnp.float32)
    for sub in range(n_sub):
        pick = jnp.where(place == rank[sub : sub + 1, :], 1.0, 0.0).astype(jnp.bfloat16)
        moved = jnp.dot(pick, grad_ref[0, sub * SUB : (sub + 1) * SUB, :], preferred_element_type=jnp.float32)
        rows_ref[pl.ds(start_ref[table, sub], SUB), :] = moved
    out_ref[0] = rows_ref[:cap, :].astype(jnp.bfloat16)


def compact_rows(by_table, lens, starts, half, cap, n_group):
    n_tab, batch, emb = by_table.shape
    n_half = (n_tab - half + 1) // 2
    return pl.pallas_call(
        functools.partial(compact_kernel, cap),
        grid=(n_half,),
        in_specs=[
            pl.BlockSpec(memory_space=pltpu.SMEM),
            pl.BlockSpec((1,) + lens.shape[1:], lambda i: (2 * i + half, 0, 0)),
            pl.BlockSpec((1, batch, emb), lambda i: (2 * i + half, 0, 0)),
        ],
        out_specs=pl.BlockSpec((1, cap, emb), lambda i: (i, 0, 0)),
        out_shape=jax.ShapeDtypeStruct((n_group, cap, emb), jnp.bfloat16),
        scratch_shapes=[pltpu.VMEM((batch + SUB, emb), jnp.float32)],
        cost_estimate=pl.CostEstimate(flops=20_000_000_000, bytes_accessed=13_000_000, transcendentals=0),
        name="compact_rows",
    )(starts[half::2], lens, by_table)


def ids_kernel(n_rows, ids_ref, len_ref, out_ref):
    shape = ids_ref.shape
    lane = lax.broadcasted_iota(jnp.int32, shape, 1)
    valid = len_ref[...] > 0
    count = valid.astype(jnp.int32)
    step = 1
    while step < shape[1]:
        count = count + jnp.where(lane >= step, pltpu.roll(count, step, 1), 0)
        step *= 2
    shift = lane + 1 - count
    packed = jnp.where(valid, ids_ref[...] + shift * (2 * n_rows), -1)
    step = 1
    while step < shape[1]:
        bit = step * 2 * n_rows
        moves = (packed & bit) != 0
        stay = jnp.where(jnp.logical_and(packed >= 0, jnp.logical_not(moves)), packed, -1)
        go = jnp.where(jnp.logical_and(packed >= 0, moves), packed, -1)
        packed = jnp.maximum(stay, pltpu.roll(go, shape[1] - step, 1))
        step *= 2
    out_ref[...] = jnp.where(packed >= 0, packed & (2 * n_rows - 1), n_rows)


def compact_ids(ids, lens, n_rows):
    return pl.pallas_call(
        functools.partial(ids_kernel, n_rows),
        out_shape=jax.ShapeDtypeStruct(ids.shape, jnp.int32),
        cost_estimate=pl.CostEstimate(flops=5_000_000_000, bytes_accessed=1_000_000, transcendentals=0),
        name="compact_ids",
    )(ids, lens)


def update_rows(acc, rate, table_ref, accum_ref, new_table_ref, new_accum_ref):
    n_blk, width = accum_ref.shape[1:]
    eye = lax.broadcasted_iota(jnp.int32, (width, width), 0) == lax.broadcasted_iota(jnp.int32, (width, width), 1)

    def block(blk, carry):
        rows = pl.ds(pl.multiple_of(blk * width, width), width)
        grad = acc[0][rows, :]
        for copy in acc[1:]:
            grad = grad + copy[rows, :]
        mean = jnp.mean(grad * grad, axis=1, keepdims=True)
        old = jnp.sum(jnp.where(eye, accum_ref[0, pl.ds(blk, 1), :], 0.0), axis=1, keepdims=True)
        new = old + mean
        scale = rate / (jnp.sqrt(new) + EPSILON)
        new_table_ref[0, rows, :] = (table_ref[0, rows, :].astype(jnp.float32) - grad * scale).astype(jnp.bfloat16)
        new_accum_ref[0, pl.ds(blk, 1), :] = jnp.sum(jnp.where(eye, new, 0.0), axis=0, keepdims=True)
        return carry

    lax.fori_loop(0, n_blk, block, 0)


def scatter_kernel(half, rate_ref, count_ref, ids_ref, recv_ref, table_ref, accum_ref, *rest):
    new_table_ref, new_accum_ref, rows_ref = rest[-(COPIES + 3) : -COPIES]
    acc = rest[-COPIES:]
    part = pl.program_id(0)

    @pl.when(part == 0)
    def _():
        for copy in acc:
            copy[...] = jnp.zeros_like(copy)

    rows_ref[...] = recv_ref[0].astype(jnp.float32)

    def step(i, carry):
        for group in range(0, ROWS, COPIES):
            base = i * ROWS + group
            where = [ids_ref[part, base + k] for k in range(COPIES)]
            total = [acc[k][pl.ds(where[k], 1), :] + rows_ref[pl.ds(base + k, 1), :] for k in range(COPIES)]
            for k in range(COPIES):
                acc[k][pl.ds(where[k], 1), :] = total[k]
        return carry

    lax.fori_loop(0, (count_ref[half, part] + (ROWS - 1)) // ROWS, step, 0)

    @pl.when(part == pl.num_programs(0) - 1)
    def _():
        update_rows(acc, rate_ref[0], table_ref, accum_ref, new_table_ref, new_accum_ref)


def scatter_update(half, recv, ids, counts, tables, accum, rate, earlier):
    n_group, cap, emb = recv.shape
    n_rows = tables.shape[1]
    slot = lambda i: (half, 0, 0)
    in_specs = [
        pl.BlockSpec(memory_space=pltpu.SMEM),
        pl.BlockSpec(memory_space=pltpu.SMEM),
        pl.BlockSpec((None,) + ids.shape[1:], slot, memory_space=pltpu.SMEM),
        pl.BlockSpec((1, cap, emb), lambda i: (i, 0, 0)),
        pl.BlockSpec((1, n_rows, emb), slot),
        pl.BlockSpec((1,) + accum.shape[1:], slot),
    ]
    args = [rate, counts, ids, recv, tables, accum]
    aliases = {}
    if earlier is not None:
        in_specs += [pl.BlockSpec(memory_space=pl.ANY)] * 2
        aliases = {len(args): 0, len(args) + 1: 1}
        args += list(earlier)
    return pl.pallas_call(
        functools.partial(scatter_kernel, half),
        grid=(n_group,),
        in_specs=in_specs,
        out_specs=[
            pl.BlockSpec((1, n_rows, emb), slot),
            pl.BlockSpec((1,) + accum.shape[1:], slot),
        ],
        out_shape=[jax.ShapeDtypeStruct(tables.shape, tables.dtype), jax.ShapeDtypeStruct(accum.shape, accum.dtype)],
        scratch_shapes=[pltpu.VMEM((cap, emb), jnp.float32)] + [pltpu.VMEM((n_rows + 8, emb), jnp.float32)] * COPIES,
        input_output_aliases=aliases,
        cost_estimate=pl.CostEstimate(flops=50_000_000_000, bytes_accessed=13_000_000, transcendentals=0),
        compiler_params=pltpu.CompilerParams(vmem_limit_bytes=60 * 1024 * 1024),
        name="scatter_update",
    )(*args)


def solution(mesh):
    n_group = mesh.shape['mp']
    slot_spec = P(('pod', 'mp'))

    def local_step(d_pool, row_ids, lengths, tables, row_accum, learn_rate):
        batch, n_tab, emb = d_pool.shape
        slots_dev, n_rows = tables.shape[:2]
        lanes = 128
        cap_fast = batch * 9 // 16

        by_source = (lengths > 0).reshape(slots_dev, n_group, batch)
        counts = jnp.sum(by_source, axis=2, dtype=jnp.int32)
        over = jnp.any(counts > cap_fast).astype(jnp.bfloat16)
        held = jnp.swapaxes(by_source, 0, 1).astype(jnp.bfloat16).reshape(n_group, -1, lanes)
        held = jnp.concatenate([held, jnp.full((n_group, 8, lanes), over)], axis=1)
        told = lax.all_to_all(held, 'mp', 0, 0, tiled=True)
        over_any = jnp.max(told[:, -1, 0]) > 0
        lens = told[:, :-8].astype(jnp.float32).reshape(n_group * slots_dev, batch // SUB, SUB)
        sub_counts = jnp.sum(lens, axis=2).astype(jnp.int32)
        starts = jnp.cumsum(sub_counts, axis=1) - sub_counts

        by_table = jnp.swapaxes(d_pool, 0, 1)
        seg_ids = row_ids.reshape(slots_dev * n_group, batch)
        ids = compact_ids(seg_ids, lengths.reshape(slots_dev * n_group, batch), n_rows)
        ids = ids.reshape(slots_dev, n_group, batch)
        accum = row_accum.reshape(slots_dev, n_rows // lanes, lanes)
        rate = learn_rate.reshape(1)

        def exchange(cap):
            done = None
            recvs = []
            for half in range(slots_dev):
                send = compact_rows(by_table, lens, starts, half, cap, n_group)
                recvs.append(lax.all_to_all(send, 'mp', 0, 0, tiled=True))
            for half in range(slots_dev):
                done = scatter_update(half, recvs[half], ids, counts, tables, accum, rate, done)
            return tuple(done)

        new_tables, new_accum = lax.cond(over_any, lambda: exchange(batch), lambda: exchange(cap_fast))
        return new_tables, new_accum.reshape(row_accum.shape)

    return jax.shard_map(local_step, mesh=mesh, in_specs=(slot_spec, slot_spec, slot_spec, slot_spec, slot_spec, P()), out_specs=(slot_spec, slot_spec), check_vma=False)
```

time: 790 us -> 333 us (0.42)
  other arithmetic: 374 us -> 5.88 us
  waiting for transfers between devices: 378 us -> 133 us
  Pallas kernels: 0 us -> 159 us
  local copies, waits for them, and re-layouts: 25.1 us -> 6.41 us
  starting transfers between devices: 10.9 us -> 25.4 us
    scatter-add x1 -> x0, other arithmetic: 351 us -> none  [add_position(): return row_grad.at[seg_rows].add(grad_vals, mode='drop')]
    all_to_all x1 -> x3, waiting for transfers between devices: 378 us -> 133 us  [the longest x2 131 us: exchange(): recvs.append(lax.all_to_all(send, 'mp', 0, 0, tiled=True))]
    pallas_call x0 -> x5, Pallas kernels: none -> 159 us  [the longest x2 130 us: scatter_update(): pl.pallas_call(functools.partial(scatter_kernel, half), grid=(n_group,),...]
    all_to_all x1 -> x3, starting transfers between devices: 10.9 us -> 25.4 us  [the longest x2 14.7 us: exchange(): recvs.append(lax.all_to_all(send, 'mp', 0, 0, tiled=True))]
    pad x1 -> x0, local copies, waits for them, and re-layouts: 13.8 us -> none  [local_step(): padded = jnp.pad(d_pool, ((0, 0), (0, slots_dev * n_group - n_tab), (0, 0)))]
    reshape x1, other arithmetic: 8.54 us -> 0.02 us  [local_step(): told[:, :-8].astype(jnp.float32)]
    convert_element_type x1, other arithmetic: 8.34 us -> 0.01 us  [local_step(): sub_counts = jnp.sum(lens, axis=2).astype(jnp.int32)]
    reshape x1 -> x4, local copies, waits for them, and re-layouts: 11 us -> 3.04 us  [the longest x1 1.87 us: local_step(): lengths.reshape(slots_dev * n_group, batch)]
  transfers between devices with their start and end apart: 1 -> 3, of which waited for: 1 -> 3; matrix products, arithmetic and copies ran while one was open for 0% -> 2% of each run, Pallas kernels for 0% -> 25%
where the time goes in v1:
time: 333 us; the launch traced here: 331 us
  Pallas kernels  159 us (48%)
  waiting for transfers between devices  133 us (40%)
  starting transfers between devices  25.4 us (8%)
  local copies, waits for them, and re-layouts  6.41 us (2%)
  other arithmetic  5.88 us (2%)
    all_to_all x2, waiting for transfers between devices, exchange(): recvs.append(lax.all_to_all(send, 'mp', 0, 0, tiled=True))  131 us
    pallas_call x2, Pallas kernels, scatter_update(): pl.pallas_call(functools.partial(scatter_kernel, half), grid=(n_group,),...  130 us
    pallas_call x2, Pallas kernels, compact_rows(): pl.pallas_call(functools.partial(compact_kernel, cap), grid=(n_half,), in...  26.4 us
    all_to_all x2, starting transfers between devices, exchange(): recvs.append(lax.all_to_all(send, 'mp', 0, 0, tiled=True))  14.7 us
    all_to_all x1, starting transfers between devices, local_step(): told = lax.all_to_all(held, 'mp', 0, 0, tiled=True)  10.7 us
  transfers between devices with their start and end apart: 3, of which 3 were waited for; matrix products, arithmetic and copies ran while one was open for 2% of the time, Pallas kernels for 25%

profile of v1, /device:TPU:21, one launch (start us, length us, event | category | flops | bytes accessed | tf_op | source)
XLA Modules:
  0.0 331.3 jit_solution(14952549418565226564)
XLA Ops:
  0.6 1.1 broadcast_compare_fusion
  1.9 0.6 compare_reduce_fusion
  2.5 0.2 reshape.53
  2.7 1.3 pad_convert_fusion
  4.1 10.7 %all-to-all-start.4 = ((bf16[16,40,128]{2,1,0:T(8,128)(2,1)}), bf16[16,40,128]{2,1,0:T(8,128)(2,1)S(1)}, u32[]{:S(2)}, u32[]{:S(2)}) async-start(bf16[16,40,128]{2,1,0:T(8,128)(2,1)} %pad_convert_fusion), calls=%async_computation.4 | async-start | bytes 327680 | tf_op jit(solution)/shard_map/all_to_all | solution.py:179
  14.8 1.9 reshape.55.len_ref
  16.7 1.7 reduce.1
  18.4 0.9 reshape.54.ids_ref
  19.3 3.2 compact_ids.1
  22.5 1.7 all-to-all-done.4
  24.6 0.6 slice_reduce_fusion
  25.9 305.5 %conditional.1 = (bf16[2,8192,128]{2,1,0:T(8,128)(2,1)}, f32[2,8192]{1,0:T(2,128)}) conditional(s32[]{:T(128)} %convert_element_type.22, (f32[]{:T(128)}, s32[32,2048]{1,0:T(8,128)S(1)}, s32[32,8]{1,0:T(8,128)S(1)}, s32[32,8]{1,0:T(8,128)S(1)}, f32[32,8,256]{2,1,0:T(8,128)S(1)}, /*index=5*/bf16[26,2048,128]{2,1,0:T(8,128)(2,1)}, ...), branch_computations={%region_5.6_spmd, %region_6.7_spmd} | conditional | flops 140000002048 | bytes 102598992 | solution.py:202
  25.9 0.6 slice.13.start_ref
  26.5 13.2 %compact_rows.5 = bf16[16,1152,128]{2,1,0:T(8,128)(2,1)} custom-call(s32[16,8]{1,0:T(8,128)} %slice.13.start_ref, f32[32,8,256]{2,1,0:T(8,128)S(1)} %get-tuple-element.54.len_ref, bf16[26,2048,128]{2,1,0:T(8,128)(2,1)} %get-tuple-element.55.grad_ref), custom_call_target="tpu_custom_call" | custom-call | flops 20000000000 | bytes 13000000 | tf_op jit(solution)/shard_map/cond/branch_0_fun/compact_rows/pallas_call | solution.py:34
  39.7 5.6 %all-to-all-start.1 = ((bf16[16,1152,128]{2,1,0:T(8,128)(2,1)}), bf16[16,1152,128]{2,1,0:T(8,128)(2,1)}, u32[]{:S(2)}, u32[]{:S(2)}) async-start(bf16[16,1152,128]{2,1,0:T(8,128)(2,1)} %compact_rows.5), calls=%async_computation.1 | async-start | bytes 9437184 | tf_op jit(solution)/shard_map/cond/branch_0_fun/all_to_all | solution.py:197
  45.3 0.6 slice.12.start_ref
  45.9 13.2 %compact_rows.4 = bf16[16,1152,128]{2,1,0:T(8,128)(2,1)} custom-call(s32[16,8]{1,0:T(8,128)} %slice.12.start_ref, f32[32,8,256]{2,1,0:T(8,128)S(1)} %get-tuple-element.54.len_ref, bf16[26,2048,128]{2,1,0:T(8,128)(2,1)} %get-tuple-element.55.grad_ref), custom_call_target="tpu_custom_call" | custom-call | flops 20000000000 | bytes 13000000 | tf_op jit(solution)/shard_map/cond/branch_0_fun/compact_rows/pallas_call | solution.py:34
  59.1 91.5 %all-to-all-done.1.recv_ref = bf16[16,1152,128]{2,1,0:T(8,128)(2,1)} async-done(((bf16[16,1152,128]{2,1,0:T(8,128)(2,1)}), bf16[16,1152,128]{2,1,0:T(8,128)(2,1)}, u32[]{:S(2)}, u32[]{:S(2)}) %all-to-all-start.1) | async-done | bytes 4718624 | tf_op jit(solution)/shard_map/cond/branch_0_fun/all_to_all | solution.py:197
  150.6 9.1 %all-to-all-start = ((bf16[16,1152,128]{2,1,0:T(8,128)(2,1)}), bf16[16,1152,128]{2,1,0:T(8,128)(2,1)}, u32[]{:S(2)}, u32[]{:S(2)}) async-start(bf16[16,1152,128]{2,1,0:T(8,128)(2,1)} %compact_rows.4), calls=%async_computation | async-start | bytes 9437184 | tf_op jit(solution)/shard_map/cond/branch_0_fun/all_to_all | solution.py:197
  159.7 0.6 copy.33
  160.3 64.9 %scatter_update.4 = (bf16[2,8192,128]{2,1,0:T(8,128)(2,1)}, f32[2,64,128]{2,1,0:T(8,128)}) custom-call(f32[1]{0:T(128)} %bitcast.rate_ref, s32[2,16]{1,0:T(2,128)S(1)} %get-tuple-element.50.count_ref, s32[2,16,2048]{2,1,0:T(8,128)S(1)} %bitcast.41, bf16[16,1152,128]{2,1,0:T(8,128)(2,1)} %all-to-all-done.1.recv_ref, ...), custom_call_target="tpu_custom_call" | custom-call | flops 49999998976 | bytes 13000000 | tf_op jit(solution)/shard_map/cond/branch_0_fun/scatter_update/pallas_call | solution.py:147
  225.2 39.8 %all-to-all-done.recv_ref = bf16[16,1152,128]{2,1,0:T(8,128)(2,1)} async-done(((bf16[16,1152,128]{2,1,0:T(8,128)(2,1)}), bf16[16,1152,128]{2,1,0:T(8,128)(2,1)}, u32[]{:S(2)}, u32[]{:S(2)}) %all-to-all-start) | async-done | bytes 4718624 | tf_op jit(solution)/shard_map/cond/branch_0_fun/all_to_all | solution.py:197
  265.0 64.9 %scatter_update.5 = (bf16[2,8192,128]{2,1,0:T(8,128)(2,1)}, f32[2,64,128]{2,1,0:T(8,128)}) custom-call(f32[1]{0:T(128)} %bitcast.rate_ref, s32[2,16]{1,0:T(2,128)S(1)} %get-tuple-element.50.count_ref, s32[2,16,2048]{2,1,0:T(8,128)S(1)} %bitcast.42, bf16[16,1152,128]{2,1,0:T(8,128)(2,1)} %all-to-all-done.recv_ref, ...), custom_call_target="tpu_custom_call", output_to_operand_aliasing={{0}: (6, {}), {1}: (7, {})} | custom-call | flops 49999998976 | bytes 13000000 | tf_op jit(solution)/shard_map/cond/branch_0_fun/scatter_update/pallas_call | solution.py:147
  329.8 1.5 copy.32
  (9 shorter events, 0.5 us)
Async XLA Ops:
  4.1 20.1 %all-to-all-start.4 = ((bf16[16,40,128]{2,1,0:T(8,128)(2,1)}), bf16[16,40,128]{2,1,0:T(8,128)(2,1)S(1)}, u32[]{:S(2)}, u32[]{:S(2)}) async-start(bf16[16,40,128]{2,1,0:T(8,128)(2,1)} %pad_convert_fusion), calls=%async_computation.4 | async-start | bytes 327680 | tf_op jit(solution)/shard_map/all_to_all | solution.py:179
  19.3 6.5 %copy-start = (f32[2,8192]{1,0:T(2,128)S(1)}, f32[2,8192]{1,0:T(2,128)}, u32[]{:S(2)}) copy-start(f32[2,8192]{1,0:T(2,128)} %param.12) | copy-start | bytes 196612
  39.7 110.9 %all-to-all-start.1 = ((bf16[16,1152,128]{2,1,0:T(8,128)(2,1)}), bf16[16,1152,128]{2,1,0:T(8,128)(2,1)}, u32[]{:S(2)}, u32[]{:S(2)}) async-start(bf16[16,1152,128]{2,1,0:T(8,128)(2,1)} %compact_rows.5), calls=%async_computation.1 | async-start | bytes 9437184 | tf_op jit(solution)/shard_map/cond/branch_0_fun/all_to_all | solution.py:197
  150.6 114.4 %all-to-all-start = ((bf16[16,1152,128]{2,1,0:T(8,128)(2,1)}), bf16[16,1152,128]{2,1,0:T(8,128)(2,1)}, u32[]{:S(2)}, u32[]{:S(2)}) async-start(bf16[16,1152,128]{2,1,0:T(8,128)(2,1)} %compact_rows.4), calls=%async_computation | async-start | bytes 9437184 | tf_op jit(solution)/shard_map/cond/branch_0_fun/all_to_all | solution.py:197
